TPU v7x, 32 devices: a whole 2x2x4 slice. The times are simulated.
32 devices in a mesh: seq: 16 (over z, y, core), head: 2 (over x).
Axes of the slice: x: 2, y: 2, z: 4, core: 2. Of those that a mesh axis runs over, the one named last changes fastest.
Arguments:
- tokens: bfloat16 [8192, 1024], P('seq'), may hold values from -24 to 24
- norm_attn: float32 [1024], replicated, may hold values from 0.5 to 1.5
- self_qkv: bfloat16 [3, 1024, 1024], P(None, None, 'head'), may hold values from -4 to 4
- self_out: bfloat16 [1024, 1024], P('head'), may hold values from -0.1875 to 0.1875
- norm_ffn: float32 [1024], replicated, may hold values from 0.5 to 1.5
- ffn_in: bfloat16 [2, 1024, 2816], P(None, None, 'head'), may hold values from -0.1875 to 0.1875
- ffn_out: bfloat16 [2816, 1024], P('head'), may hold values from -0.109375 to 0.109375
- norm_final: float32 [1024], replicated, may hold values from 0.5 to 1.5
- pad_lengths: int32 [16], replicated, may hold values from 64 to 512
- targets: bfloat16 [512, 1024], replicated, may hold values from -8 to 8
- target_lengths: int32 [4], replicated, may hold values from 32 to 128
- norm_cross: float32 [1024], replicated, may hold values from 0.1 to 1.9
- cross_query: bfloat16 [1024, 1024], P(None, 'head'), may hold values from -4 to 4
- cross_kv: bfloat16 [2, 1024, 1024], P(None, None, 'head'), may hold values from -4 to 4
- cross_out: bfloat16 [1024, 1024], P('head'), may hold values from -4 to 4
Outputs:
- encoded: bfloat16 [8192, 1024], P('seq')
- decoded: bfloat16 [512, 1024], replicated
All inputs are finite; a program needn't handle non-finite values.
Results may differ from a plain program's by a relative error of at most 0.033.
Values may be sent and summed in bfloat16 or wider, within the bound.
A program may use at most 128 MiB of HBM per device.

v0:
```python
import math
import jax
import jax.numpy as jnp
from jax import lax
from jax.sharding import PartitionSpec as P

HD = 64
TOK_DEV = 512
TGT_LEN = 128
epsilon = 1e-06
masked_score = -1e30


def rms_norm(values, gain_vector):
    widened = values.astype(jnp.float32)
    return (
        widened
        * lax.rsqrt(jnp.mean(widened * widened, axis=-1, keepdims=True) + epsilon)
        * gain_vector
    )


def spread_heads(per_head):
    return jnp.repeat(per_head.T, HD, axis=1)


def live_within(positions, lengths, span):
    block_ids = jnp.arange(lengths.shape[0], dtype=jnp.int32)
    owners = positions // span
    lengths_here = jnp.sum(
        jnp.where(owners[:, None] == block_ids[None, :], lengths[None, :], 0), axis=1
    )
    return positions % span < lengths_here


def live_keys(positions, pad_lengths):
    return live_within(positions, pad_lengths, TOK_DEV)


def flash_block(flash_state, query_heads, key_rows, value_rows, live_rows, scaling):
    running_max, running_sum, running_acc = flash_state
    key_count = key_rows.shape[0]
    heads_here = query_heads.shape[1]
    keys_split = key_rows.reshape(key_count, heads_here, HD)
    values_split = value_rows.reshape(key_count, heads_here, HD)
    scores = (
        jnp.einsum("qhd,khd->hqk", query_heads, keys_split, preferred_element_type=jnp.float32)
        * scaling
    )
    scores = jnp.where(live_rows[None, None, :], scores, masked_score)
    new_max = jnp.maximum(running_max, jnp.max(scores, axis=-1))
    shrink = jnp.exp(running_max - new_max)
    weights = jnp.where(live_rows[None, None, :], jnp.exp(scores - new_max[:, :, None]), 0.0)
    new_sum = running_sum * shrink + jnp.sum(weights, axis=-1)
    mixed_values = jnp.einsum(
        "hqk,khd->qhd",
        weights.astype(jnp.bfloat16),
        values_split,
        preferred_element_type=jnp.float32,
    )
    new_acc = running_acc * spread_heads(shrink) + mixed_values.reshape(
        mixed_values.shape[0], heads_here * HD
    )
    return (new_max, new_sum, new_acc)


def feed_forward(normed_in, ffn_in, ffn_out):
    gate_proj = jnp.dot(normed_in, ffn_in[0], preferred_element_type=jnp.float32)
    up_proj = jnp.dot(normed_in, ffn_in[1], preferred_element_type=jnp.float32)
    activated = (jax.nn.gelu(gate_proj, approximate=True) * up_proj).astype(jnp.bfloat16)
    return jnp.dot(activated, ffn_out, preferred_element_type=jnp.float32)


def local(
    tokens,
    norm_attn,
    self_qkv,
    self_out,
    norm_ffn,
    ffn_in,
    ffn_out,
    norm_final,
    pad_lengths,
    targets,
    target_lengths,
    norm_cross,
    cross_query,
    cross_kv,
    cross_out,
):
    row_count = tokens.shape[0]
    heads_here = self_qkv.shape[2] // HD
    scaling = HD ** (-0.5)
    normed = rms_norm(tokens, norm_attn).astype(jnp.bfloat16)
    queries = jnp.dot(normed, self_qkv[0], preferred_element_type=jnp.float32).astype(jnp.bfloat16)
    keys_local = jnp.dot(normed, self_qkv[1], preferred_element_type=jnp.float32).astype(
        jnp.bfloat16
    )
    values_local = jnp.dot(normed, self_qkv[2], preferred_element_type=jnp.float32).astype(
        jnp.bfloat16
    )
    query_heads = queries.reshape(row_count, heads_here, HD)
    start_state = (
        jnp.full((heads_here, row_count), masked_score, jnp.float32),
        jnp.zeros((heads_here, row_count), jnp.float32),
        jnp.zeros((row_count, heads_here * HD), jnp.float32),
    )
    key_piece = lax.all_gather(keys_local, "seq", axis=0, tiled=True)
    value_piece = lax.all_gather(values_local, "seq", axis=0, tiled=True)
    piece_rows = key_piece.shape[0]
    block_width = math.gcd(piece_rows, 2048)

    def step_once(inner_state, block_index):
        first_row = block_index * block_width
        key_rows = lax.dynamic_slice_in_dim(key_piece, first_row, block_width, 0)
        value_rows = lax.dynamic_slice_in_dim(value_piece, first_row, block_width, 0)
        positions = first_row + jnp.arange(block_width, dtype=jnp.int32)
        updated = flash_block(
            inner_state,
            query_heads,
            key_rows,
            value_rows,
            live_keys(positions, pad_lengths),
            scaling,
        )
        return (updated, None)

    final_state, unused = lax.scan(
        step_once, start_state, jnp.arange(piece_rows // block_width, dtype=jnp.int32)
    )
    final_max, final_sum, final_acc = final_state
    context = (final_acc / spread_heads(final_sum)).astype(jnp.bfloat16)
    attn_part = jnp.dot(context, self_out, preferred_element_type=jnp.float32)
    hidden_in = tokens.astype(jnp.float32) + lax.psum(
        attn_part.astype(jnp.bfloat16), "head"
    ).astype(jnp.float32)
    ffn_normed = rms_norm(hidden_in, norm_ffn).astype(jnp.bfloat16)
    ffn_part = feed_forward(ffn_normed, ffn_in, ffn_out)
    final_in = hidden_in + lax.psum(ffn_part.astype(jnp.bfloat16), "head").astype(jnp.float32)
    encoded = rms_norm(final_in, norm_final).astype(jnp.bfloat16)
    target_rows = targets.shape[0]
    cross_normed = rms_norm(targets, norm_cross).astype(jnp.bfloat16)
    cross_queries = jnp.dot(cross_normed, cross_query, preferred_element_type=jnp.float32).astype(
        jnp.bfloat16
    )
    cross_keys = jnp.dot(encoded, cross_kv[0], preferred_element_type=jnp.float32).astype(
        jnp.bfloat16
    )
    cross_values = jnp.dot(encoded, cross_kv[1], preferred_element_type=jnp.float32).astype(
        jnp.bfloat16
    )
    cross_heads = cross_queries.reshape(target_rows, heads_here, HD)
    keys_split = cross_keys.reshape(row_count, heads_here, HD)
    values_split = cross_values.reshape(row_count, heads_here, HD)
    positions = lax.axis_index("seq") * row_count + jnp.arange(row_count, dtype=jnp.int32)
    live_here = live_keys(positions, pad_lengths)
    cross_scores = (
        jnp.einsum("qhd,khd->hqk", cross_heads, keys_split, preferred_element_type=jnp.float32)
        * scaling
    )
    cross_scores = jnp.where(live_here[None, None, :], cross_scores, masked_score)
    local_max = jnp.max(cross_scores, axis=-1)
    global_max = lax.pmax(local_max, "seq")
    weights = jnp.where(
        live_here[None, None, :], jnp.exp(cross_scores - global_max[:, :, None]), 0.0
    )
    local_sum = jnp.sum(weights, axis=-1)
    local_mixed = jnp.einsum(
        "hqk,khd->qhd",
        weights.astype(jnp.bfloat16),
        values_split,
        preferred_element_type=jnp.float32,
    )
    weight_sum, mixed_values = (
        lax.psum(local_sum.astype(jnp.bfloat16), "seq").astype(jnp.float32),
        lax.psum(
            local_mixed.reshape(target_rows, heads_here * HD).astype(jnp.bfloat16), "seq"
        ).astype(jnp.float32),
    )
    cross_context = (mixed_values / spread_heads(weight_sum)).astype(jnp.bfloat16)
    cross_part = jnp.dot(cross_context, cross_out, preferred_element_type=jnp.float32)
    cross_total = lax.psum(cross_part.astype(jnp.bfloat16), "head").astype(jnp.float32)
    slots = jnp.arange(target_rows, dtype=jnp.int32)
    target_live = slots % TGT_LEN < jnp.repeat(
        target_lengths, TGT_LEN, total_repeat_length=target_rows
    )
    decoded = (
        targets.astype(jnp.float32) + jnp.where(target_live[:, None], cross_total, 0.0)
    ).astype(jnp.bfloat16)
    return (encoded, decoded)


def solution(mesh):
    placed = (
        P("seq", None),
        P(),
        P(None, None, "head"),
        P("head", None),
        P(),
        P(None, None, "head"),
        P("head", None),
        P(),
        P(),
        P(),
        P(),
        P(),
        P(None, "head"),
        P(None, None, "head"),
        P("head", None),
    )
    return jax.shard_map(
        local, mesh=mesh, in_specs=placed, out_specs=(P("seq", None), P()), check_vma=False
    )
```

profile of v0, /device:TPU:0, one launch (start us, length us, event | category | flops | bytes accessed | tf_op | source)
XLA Modules:
  0.0 726.6 jit_solution(55890220503606311)
XLA Ops:
  17.7 71.5 %all-gather.3.cloned.1.call-done = bf16[8192,512]{1,0:T(8,128)(2,1)} async-done(((bf16[512,512]{1,0:T(8,128)(2,1)}), bf16[8192,512]{1,0:T(8,128)(2,1)}) %all-gather.3.cloned.1.call-update) | async-done | bytes 8388624 | tf_op jit(solution)/shard_map/all_gather | solution.py:108
  89.2 75.1 %all-gather.5.cloned.1.call-done = bf16[8192,512]{1,0:T(8,128)(2,1)} async-done(((bf16[512,512]{1,0:T(8,128)(2,1)}), bf16[8192,512]{1,0:T(8,128)(2,1)}) %all-gather.5.cloned.1.call-update) | async-done | bytes 8388624 | tf_op jit(solution)/shard_map/all_gather | solution.py:109
  164.3 242.0 %while.18 = (s32[]{:T(128)}, f32[8,512]{1,0:T(8,128)S(1)}, f32[8,512]{1,0:T(8,128)S(1)}, f32[512,512]{0,1:T(8,128)}, s32[4]{0:T(128)S(1)}, /*index=5*/s32[16]{0:...) while((s32[]{:T(128)}, f32[8,512]{1,0:T(8,128)S(1)}, ...), condition=%wide.region_5.6_spmd.clone, body=%wide.region_1.5_spmd.clone.sunk | while | flops 2257502208 | bytes 135045456 | solution.py:128
  165.5 4.5 constant_dynamic-slice_fusion.3
  174.1 15.6 %bitcast_reduce_fusion.2 = (f32[8,512]{1,0:T(8,128)S(1)}, f32[8,2048,512]{2,1,0:T(8,128)}) fusion(pred[2048]{0:T(1024)(128)(4,1)S(1)} %fusion.113, bf16[2048,8,64]{0,2,1:T(8,128)(2,1)} %bitcast.120, bf16[512,8,64]{0,2,1:T(8,128)(2,1)S(1)} %get-tuple-element.311), kind=kOutput, calls=%fused_computation.1.clone.1 | convolution fusion | flops 1098903552 | bytes 36194304 | tf_op jit(solution)/shard_map/while/body/eval_jaxpr/qhd,khd->hqk/dot_general | solution.py:47
  189.7 4.0 copy.32
  193.7 14.9 %fusion.117 = f32[8,64,512]{2,1,0:T(8,128)S(1)} fusion(bf16[2048,8,64]{0,2,1:T(8,128)(2,1)} %bitcast.121, f32[8,2048,512]{2,1,0:T(8,128)} %get-tuple-element.275, f32[8,512]{1,0:T(8,128)S(1)} %get-tuple-element.305, pred[2048]{0:T(1024)(128)(4,1)S(1)} %fusion.113), kind=kOutput, calls=%fused_computation.7.clone.1 | convolution fusion | flops 1115684864 | bytes 36718592 | tf_op jit(solution)/shard_map/while/body/eval_jaxpr/hqk,khd->qhd/dot_general | solution.py:55
  209.0 15.7 %fusion.115 = f32[8,512]{1,0:T(8,128)S(1)} fusion(f32[8,2048,512]{2,1,0:T(8,128)} %get-tuple-element.275, f32[8,512]{1,0:T(8,128)S(1)} %get-tuple-element.305, pred[2048]{0:T(1024)(128)(4,1)S(1)} %fusion.113), kind=kLoop, calls=%fused_computation.6.clone.1 | loop fusion | flops 41938944 | bytes 33589248 | tf_op jit(solution)/shard_map/while/body/eval_jaxpr/reduce_sum | solution.py:54
  226.0 4.5 constant_dynamic-slice_fusion.3
  234.6 15.6 %bitcast_reduce_fusion.2 = (f32[8,512]{1,0:T(8,128)S(1)}, f32[8,2048,512]{2,1,0:T(8,128)}) fusion(pred[2048]{0:T(1024)(128)(4,1)S(1)} %fusion.113, bf16[2048,8,64]{0,2,1:T(8,128)(2,1)} %bitcast.120, bf16[512,8,64]{0,2,1:T(8,128)(2,1)S(1)} %get-tuple-element.311), kind=kOutput, calls=%fused_computation.1.clone.1 | convolution fusion | flops 1098903552 | bytes 36194304 | tf_op jit(solution)/shard_map/while/body/eval_jaxpr/qhd,khd->hqk/dot_general | solution.py:47
  250.3 4.0 copy.32
  254.2 14.9 %fusion.117 = f32[8,64,512]{2,1,0:T(8,128)S(1)} fusion(bf16[2048,8,64]{0,2,1:T(8,128)(2,1)} %bitcast.121, f32[8,2048,512]{2,1,0:T(8,128)} %get-tuple-element.275, f32[8,512]{1,0:T(8,128)S(1)} %get-tuple-element.305, pred[2048]{0:T(1024)(128)(4,1)S(1)} %fusion.113), kind=kOutput, calls=%fused_computation.7.clone.1 | convolution fusion | flops 1115684864 | bytes 36718592 | tf_op jit(solution)/shard_map/while/body/eval_jaxpr/hqk,khd->qhd/dot_general | solution.py:55
  269.5 15.7 %fusion.115 = f32[8,512]{1,0:T(8,128)S(1)} fusion(f32[8,2048,512]{2,1,0:T(8,128)} %get-tuple-element.275, f32[8,512]{1,0:T(8,128)S(1)} %get-tuple-element.305, pred[2048]{0:T(1024)(128)(4,1)S(1)} %fusion.113), kind=kLoop, calls=%fused_computation.6.clone.1 | loop fusion | flops 41938944 | bytes 33589248 | tf_op jit(solution)/shard_map/while/body/eval_jaxpr/reduce_sum | solution.py:54
  286.6 4.5 constant_dynamic-slice_fusion.3
  295.1 15.6 %bitcast_reduce_fusion.2 = (f32[8,512]{1,0:T(8,128)S(1)}, f32[8,2048,512]{2,1,0:T(8,128)}) fusion(pred[2048]{0:T(1024)(128)(4,1)S(1)} %fusion.113, bf16[2048,8,64]{0,2,1:T(8,128)(2,1)} %bitcast.120, bf16[512,8,64]{0,2,1:T(8,128)(2,1)S(1)} %get-tuple-element.311), kind=kOutput, calls=%fused_computation.1.clone.1 | convolution fusion | flops 1098903552 | bytes 36194304 | tf_op jit(solution)/shard_map/while/body/eval_jaxpr/qhd,khd->hqk/dot_general | solution.py:47
  314.7 14.9 %fusion.117 = f32[8,64,512]{2,1,0:T(8,128)S(1)} fusion(bf16[2048,8,64]{0,2,1:T(8,128)(2,1)} %bitcast.121, f32[8,2048,512]{2,1,0:T(8,128)} %get-tuple-element.275, f32[8,512]{1,0:T(8,128)S(1)} %get-tuple-element.305, pred[2048]{0:T(1024)(128)(4,1)S(1)} %fusion.113), kind=kOutput, calls=%fused_computation.7.clone.1 | convolution fusion | flops 1115684864 | bytes 36718592 | tf_op jit(solution)/shard_map/while/body/eval_jaxpr/hqk,khd->qhd/dot_general | solution.py:55
  330.1 15.7 %fusion.115 = f32[8,512]{1,0:T(8,128)S(1)} fusion(f32[8,2048,512]{2,1,0:T(8,128)} %get-tuple-element.275, f32[8,512]{1,0:T(8,128)S(1)} %get-tuple-element.305, pred[2048]{0:T(1024)(128)(4,1)S(1)} %fusion.113), kind=kLoop, calls=%fused_computation.6.clone.1 | loop fusion | flops 41938944 | bytes 33589248 | tf_op jit(solution)/shard_map/while/body/eval_jaxpr/reduce_sum | solution.py:54
  347.1 4.5 constant_dynamic-slice_fusion.3
  355.7 15.6 %bitcast_reduce_fusion.2 = (f32[8,512]{1,0:T(8,128)S(1)}, f32[8,2048,512]{2,1,0:T(8,128)}) fusion(pred[2048]{0:T(1024)(128)(4,1)S(1)} %fusion.113, bf16[2048,8,64]{0,2,1:T(8,128)(2,1)} %bitcast.120, bf16[512,8,64]{0,2,1:T(8,128)(2,1)S(1)} %get-tuple-element.311), kind=kOutput, calls=%fused_computation.1.clone.1 | convolution fusion | flops 1098903552 | bytes 36194304 | tf_op jit(solution)/shard_map/while/body/eval_jaxpr/qhd,khd->hqk/dot_general | solution.py:47
  375.3 14.9 %fusion.117 = f32[8,64,512]{2,1,0:T(8,128)S(1)} fusion(bf16[2048,8,64]{0,2,1:T(8,128)(2,1)} %bitcast.121, f32[8,2048,512]{2,1,0:T(8,128)} %get-tuple-element.275, f32[8,512]{1,0:T(8,128)S(1)} %get-tuple-element.305, pred[2048]{0:T(1024)(128)(4,1)S(1)} %fusion.113), kind=kOutput, calls=%fused_computation.7.clone.1 | convolution fusion | flops 1115684864 | bytes 36718592 | tf_op jit(solution)/shard_map/while/body/eval_jaxpr/hqk,khd->qhd/dot_general | solution.py:55
  390.6 15.7 %fusion.115 = f32[8,512]{1,0:T(8,128)S(1)} fusion(f32[8,2048,512]{2,1,0:T(8,128)} %get-tuple-element.275, f32[8,512]{1,0:T(8,128)S(1)} %get-tuple-element.305, pred[2048]{0:T(1024)(128)(4,1)S(1)} %fusion.113), kind=kLoop, calls=%fused_computation.6.clone.1 | loop fusion | flops 41938944 | bytes 33589248 | tf_op jit(solution)/shard_map/while/body/eval_jaxpr/reduce_sum | solution.py:54
  410.9 38.6 %all-reduce.5.cloned.1.call-done = bf16[512,1024]{1,0:T(8,128)(2,1)} async-done(((bf16[512,1024]{1,0:T(8,128)(2,1)}), bf16[512,1024]{1,0:T(8,128)(2,1)}) %all-reduce.5.cloned.1.call-update) | async-done | bytes 1048592 | tf_op jit(solution)/shard_map/psum | solution.py:134
  451.5 5.9 fusion.34
  457.4 7.9 %convolution_convert_fusion = bf16[512,1024]{1,0:T(8,128)(2,1)} fusion(bf16[1408,1024]{1,0:T(8,128)(2,1)S(1)} %copy-done, f32[512,1408]{1,0:T(8,128)} %fusion.34, bf16[2,1024,1408]{2,1,0:T(8,128)(2,1)} %param.24, bf16[512,1024]{1,0:T(8,128)(2,1)} %all-reduce.5.cloned.1.call-done, bf16[512,1024]{1,0:T(8,128)(2,1)} %param.19, f32[1024]{0:T(1024)S(1)} %copy-done.12, ...), kind=kOutput, calls=%fused_computation.77 | convolution fusion | flops 2963668992 | bytes 11802624 | tf_op jit(solution)/shard_map/dot_general | solution.py:71
  469.4 36.1 %all-reduce.7.cloned.1.call-done = bf16[512,1024]{1,0:T(8,128)(2,1)} async-done(((bf16[512,1024]{1,0:T(8,128)(2,1)}), bf16[512,1024]{1,0:T(8,128)(2,1)}) %all-reduce.7.cloned.1.call-update) | async-done | bytes 1048592 | tf_op jit(solution)/shard_map/psum | solution.py:139
  512.1 5.2 fusion.19
  517.2 61.0 %pmax.7 = f32[8,512]{1,0:T(8,128)S(1)} all-reduce(f32[8,512]{1,0:T(8,128)S(1)} %get-tuple-element.209), channel_id=1, replica_groups=mesh['seq'=16,'head'=2] {'seq'}, use_global_device_ids=true, to_apply=%region_13.14 | all-reduce | flops 4096 | bytes 32768 | tf_op jit(solution)/shard_map/pmax | solution.py:163
  578.2 6.4 fusion.45
  584.8 4.7 fusion.20
  589.4 30.1 %psum.38 = bf16[512,8]{0,1:T(8,128)(2,1)S(1)} all-reduce(bf16[512,8]{0,1:T(8,128)(2,1)S(1)} %bitcast.127), channel_id=1, replica_groups=mesh['seq'=16,'head'=2] {'seq'}, use_global_device_ids=true, to_apply=%region_16.17 | all-reduce | flops 4096 | bytes 16384 | tf_op jit(solution)/shard_map/psum | solution.py:175
  619.6 52.5 %all-reduce.9.cloned.1.call-done = bf16[512,512]{0,1:T(8,128)(2,1)} async-done(((bf16[512,512]{0,1:T(8,128)(2,1)}), bf16[512,512]{0,1:T(8,128)(2,1)}) %all-reduce.9.cloned.1.call-update) | async-done | bytes 524304 | tf_op jit(solution)/shard_map/psum | solution.py:176
  679.4 37.5 %all-reduce.11.cloned.1.call-done = bf16[512,1024]{1,0:T(8,128)(2,1)} async-done(((bf16[512,1024]{1,0:T(8,128)(2,1)}), bf16[512,1024]{1,0:T(8,128)(2,1)}) %all-reduce.11.cloned.1.call-update) | async-done | bytes 1048592 | tf_op jit(solution)/shard_map/psum | solution.py:182
  (123 shorter events, 65.9 us)
Async XLA Ops:
  7.2 450.2 %copy-start = (bf16[1408,1024]{1,0:T(8,128)(2,1)S(1)}, bf16[1408,1024]{1,0:T(8,128)(2,1)}, u32[]{:S(2)}) copy-start(bf16[1408,1024]{1,0:T(8,128)(2,1)} %param.25) | copy-start | bytes 8650756
  7.2 4.9 copy-start.11
  7.2 82.0 %all-gather.3.cloned.1.call-start = ((), (), s32[]{:S(2)}) async-start(), calls=%async_computation | async-start | bytes 8912896 | tf_op jit(solution)/shard_map/all_gather | solution.py:108
  12.0 152.3 %all-gather.5.cloned.1.call-start = ((), (), s32[]{:S(2)}) async-start(), calls=%async_computation.1 | async-start | bytes 8912896 | tf_op jit(solution)/shard_map/all_gather | solution.py:109
  15.2 149.1 %copy-start.7 = (s32[16]{0:T(128)S(1)}, s32[16]{0:T(128)}, u32[]{:S(2)}) copy-start(s32[16]{0:T(128)} %param.27) | copy-start | bytes 196
  15.2 434.3 %all-reduce.5.cloned.1.call-start = ((), (), s32[]{:S(2)}) async-start(), calls=%async_computation.2 | async-start | bytes 2097152 | tf_op jit(solution)/shard_map/psum | solution.py:134
  193.7 14.9 %copy-start.1 = (f32[512,512]{0,1:T(8,128)S(1)}, f32[512,512]{0,1:T(8,128)}, u32[]{:S(2)}) copy-start(f32[512,512]{0,1:T(8,128)} %get-tuple-element.294) | copy-start | bytes 3145732 | tf_op jit(solution)/shard_map/while
  209.0 15.7 %copy-start.2 = (f32[512,512]{0,1:T(8,128)}, f32[512,512]{0,1:T(8,128)S(1)}, u32[]{:S(2)}) copy-start(f32[512,512]{0,1:T(8,128)S(1)} %bitcast_add_fusion.2) | copy-start | bytes 3145732 | tf_op jit(solution)/shard_map/while
  254.2 14.9 %copy-start.1 = (f32[512,512]{0,1:T(8,128)S(1)}, f32[512,512]{0,1:T(8,128)}, u32[]{:S(2)}) copy-start(f32[512,512]{0,1:T(8,128)} %get-tuple-element.294) | copy-start | bytes 3145732 | tf_op jit(solution)/shard_map/while
  269.5 15.7 %copy-start.2 = (f32[512,512]{0,1:T(8,128)}, f32[512,512]{0,1:T(8,128)S(1)}, u32[]{:S(2)}) copy-start(f32[512,512]{0,1:T(8,128)S(1)} %bitcast_add_fusion.2) | copy-start | bytes 3145732 | tf_op jit(solution)/shard_map/while
  314.7 14.9 %copy-start.1 = (f32[512,512]{0,1:T(8,128)S(1)}, f32[512,512]{0,1:T(8,128)}, u32[]{:S(2)}) copy-start(f32[512,512]{0,1:T(8,128)} %get-tuple-element.294) | copy-start | bytes 3145732 | tf_op jit(solution)/shard_map/while
  330.0 15.7 %copy-start.2 = (f32[512,512]{0,1:T(8,128)}, f32[512,512]{0,1:T(8,128)S(1)}, u32[]{:S(2)}) copy-start(f32[512,512]{0,1:T(8,128)S(1)} %bitcast_add_fusion.2) | copy-start | bytes 3145732 | tf_op jit(solution)/shard_map/while
  375.3 14.9 %copy-start.1 = (f32[512,512]{0,1:T(8,128)S(1)}, f32[512,512]{0,1:T(8,128)}, u32[]{:S(2)}) copy-start(f32[512,512]{0,1:T(8,128)} %get-tuple-element.294) | copy-start | bytes 3145732 | tf_op jit(solution)/shard_map/while
  390.6 15.7 %copy-start.2 = (f32[512,512]{0,1:T(8,128)}, f32[512,512]{0,1:T(8,128)S(1)}, u32[]{:S(2)}) copy-start(f32[512,512]{0,1:T(8,128)S(1)} %bitcast_add_fusion.2) | copy-start | bytes 3145732 | tf_op jit(solution)/shard_map/while
  407.7 43.8 %copy-start.12 = (f32[1024]{0:T(1024)S(1)}, f32[1024]{0:T(1024)}, u32[]{:S(2)}) copy-start(f32[1024]{0:T(1024)} %param.23) | copy-start | bytes 12292
  410.6 94.9 %all-reduce.7.cloned.1.call-start = ((), (), s32[]{:S(2)}) async-start(), calls=%async_computation.3 | async-start | bytes 2097152 | tf_op jit(solution)/shard_map/psum | solution.py:139
  457.4 9.6 %copy-start.13 = (f32[1024]{0:T(1024)S(1)}, f32[1024]{0:T(1024)}, u32[]{:S(2)}) copy-start(f32[1024]{0:T(1024)} %param.30) | copy-start | bytes 12292
  465.3 206.8 %all-reduce.9.cloned.1.call-start = ((), (), s32[]{:S(2)}) async-start(), calls=%async_computation.4 | async-start | bytes 1048576 | tf_op jit(solution)/shard_map/psum | solution.py:176
  467.0 41.1 %copy-start.9 = (f32[1024]{0:T(1024)S(1)}, f32[1024]{0:T(1024)}, u32[]{:S(2)}) copy-start(f32[1024]{0:T(1024)} %param.26) | copy-start | bytes 12292
  505.5 2.6 copy-start.3
  505.5 2.6 copy-start.4
  505.5 2.8 copy-start.5
  508.1 1.7 copy-start.10
  509.7 2.3 copy-start.6
  584.7 132.2 %all-reduce.11.cloned.1.call-start = ((), (), s32[]{:S(2)}) async-start(), calls=%async_computation.5 | async-start | bytes 2097152 | tf_op jit(solution)/shard_map/psum | solution.py:182
  589.4 86.8 %copy-start.8 = (s32[4]{0:T(128)S(1)}, s32[4]{0:T(128)}, u32[]{:S(2)}) copy-start(s32[4]{0:T(128)} %param.29) | copy-start | bytes 52
Sparse Core Ops, SparseCore 0:
  12.2 77.0 all-gather.2
  91.4 72.8 all-gather.4
  410.8 38.6 all-reduce.4
  465.4 40.0 all-reduce.6
  584.8 87.1 all-reduce.8
  676.3 40.5 all-reduce.10
where the time goes:
time: 728 us; the launch traced here: 727 us
  waiting for transfers between devices  311 us (43%)
  matrix products  167 us (23%)
  blocking collectives  91.1 us (13%)
  other arithmetic  85.7 us (12%)
  local copies, waits for them, and re-layouts  53.9 us (7%)
  between operations  14.4 us (2%)
    all_gather x1, waiting for transfers between devices, local(): value_piece = lax.all_gather(values_local, 'seq', axis=0, tiled=True)  75.1 us
    all_gather x1, waiting for transfers between devices, local(): key_piece = lax.all_gather(keys_local, 'seq', axis=0, tiled=True)  71.5 us
    reduce_sum x4, other arithmetic, flash_block(): new_sum = running_sum * shrink + jnp.sum(weights, axis=-1)  62.8 us
    dot_general x4, matrix products, flash_block(): jnp.einsum('qhd,khd->hqk', query_heads, keys_split, preferred_element_typ...  62.5 us
    pmax x1, blocking collectives, local(): global_max = lax.pmax(local_max, 'seq')  61 us
    dot_general x4, matrix products, flash_block(): jnp.einsum('hqk,khd->qhd', weights.astype(jnp.bfloat16), values_split, pr...  59.7 us
    psum x1, waiting for transfers between devices, local(): lax.psum(local_mixed.reshape(target_rows, heads_here * HD).astype(jnp.bfl...  52.5 us
    psum x1, waiting for transfers between devices, local(): lax.psum(attn_part.astype(jnp.bfloat16), 'head').astype(jnp.float32)  38.6 us
  transfers between devices with their start and end apart: 6, of which 6 were waited for; matrix products, arithmetic and copies ran while one was open for 2% of the time, Pallas kernels for 0%

commit v1 on v0

--- a/solution.py
+++ b/solution.py
@@ -105,8 +105,13 @@
         jnp.zeros((heads_here, row_count), jnp.float32),
         jnp.zeros((row_count, heads_here * HD), jnp.float32),
     )
-    key_piece = lax.all_gather(keys_local, "seq", axis=0, tiled=True)
-    value_piece = lax.all_gather(values_local, "seq", axis=0, tiled=True)
+    key_piece, value_piece = jnp.split(
+        lax.all_gather(
+            jnp.concatenate([keys_local, values_local], axis=1), axis_name="seq", axis=0, tiled=True
+        ),
+        [keys_local.shape[1]],
+        axis=1,
+    )
     piece_rows = key_piece.shape[0]
     block_width = math.gcd(piece_rows, 2048)
 

time: 728 us -> 683 us (0.938)
  local copies, waits for them, and re-layouts: 53.9 us -> 31.7 us
  waiting for transfers between devices: 311 us -> 295 us
    dynamic_slice x8 -> x4, local copies, waits for them, and re-layouts: 33.8 us -> 15.9 us  [step_once(): lax.dynamic_slice_in_dim(value_piece, first_row, block_width, 0)]
    all_gather x2 -> x1, waiting for transfers between devices: 147 us -> 130 us  [local(): lax.all_gather(jnp.concatenate([keys_local, values_local], axis=1), axis_...]
    dynamic_slice x4 -> x0, local copies, waits for them, and re-layouts: 15.9 us -> none  [step_once(): key_rows = lax.dynamic_slice_in_dim(key_piece, first_row, block_width, 0)]
    split x0 -> x1, local copies, waits for them, and re-layouts: none -> 11.6 us  [local(): jnp.split(lax.all_gather(jnp.concatenate([keys_local, values_local], axis...]
  transfers between devices with their start and end apart: 6 -> 5, of which waited for: 6 -> 5; matrix products, arithmetic and copies ran while one was open for 2% -> 2% of each run, Pallas kernels for 0% -> 0%
where the time goes in v1:
time: 683 us; the launch traced here: 682 us
  waiting for transfers between devices  295 us (43%)
  matrix products  160 us (23%)
  blocking collectives  91.1 us (13%)
  other arithmetic  86.8 us (13%)
  local copies, waits for them, and re-layouts  31.7 us (5%)
  between operations  14.1 us (2%)
    all_gather x1, waiting for transfers between devices, local(): lax.all_gather(jnp.concatenate([keys_local, values_local], axis=1), axis_...  130 us
    reduce_sum x4, other arithmetic, flash_block(): new_sum = running_sum * shrink + jnp.sum(weights, axis=-1)  62.8 us
    pmax x1, blocking collectives, local(): global_max = lax.pmax(local_max, 'seq')  61 us
    dot_general x4, matrix products, flash_block(): jnp.einsum('hqk,khd->qhd', weights.astype(jnp.bfloat16), values_split, pr...  59.9 us
    dot_general x4, matrix products, flash_block(): jnp.einsum('qhd,khd->hqk', query_heads, keys_split, preferred_element_typ...  57.7 us
    psum x1, waiting for transfers between devices, local(): lax.psum(local_mixed.reshape(target_rows, heads_here * HD).astype(jnp.bfl...  52.5 us
    psum x1, waiting for transfers between devices, local(): lax.psum(attn_part.astype(jnp.bfloat16), 'head').astype(jnp.float32)  38.2 us
    psum x1, waiting for transfers between devices, local(): lax.psum(cross_part.astype(jnp.bfloat16), 'head').astype(jnp.float32)  37.5 us
  transfers between devices with their start and end apart: 5, of which 5 were waited for; matrix products, arithmetic and copies ran while one was open for 2% of the time, Pallas kernels for 0%

profile of v1, /device:TPU:0, one launch (start us, length us, event | category | flops | bytes accessed | tf_op | source)
XLA Modules:
  0.0 682.1 jit_solution(8168460260050811754)
XLA Ops:
  17.0 130.3 %all-gather.2.cloned.1.call-done = bf16[8192,1024]{0,1:T(8,128)(2,1)} async-done(((bf16[512,1024]{0,1:T(8,128)(2,1)}), bf16[8192,1024]{0,1:T(8,128)(2,1)}) %all-gather.2.cloned.1.call-update) | async-done | bytes 16777232 | tf_op jit(solution)/shard_map/all_gather | solution.py:109
  147.3 11.6 %fusion.85 = (bf16[8192,512]{0,1:T(8,128)(2,1)}, bf16[8192,512]{0,1:T(8,128)(2,1)}) fusion(bf16[8192,1024]{0,1:T(8,128)(2,1)} %all-gather.2.cloned.1.call-done), kind=kLoop, calls=%fused_computation.143 | loop fusion | bytes 33554432 | tf_op jit(solution)/shard_map/split | solution.py:108
  158.8 203.7 %while.18 = (s32[]{:T(128)}, f32[8,512]{1,0:T(8,128)S(1)}, f32[8,512]{1,0:T(8,128)S(1)}, f32[512,512]{0,1:T(8,128)}, s32[4]{0:T(128)S(1)}, /*index=5*/s32[16]{0:...) while((s32[]{:T(128)}, f32[8,512]{1,0:T(8,128)S(1)}, ...), condition=%wide.region_5.6_spmd.clone, body=%wide.region_1.5_spmd.clone.sunk | while | flops 2257502208 | bytes 126656840 | solution.py:133
  160.1 4.0 constant_dynamic-slice_fusion.3
  164.2 14.4 %bitcast_reduce_fusion.2 = (f32[8,512]{1,0:T(8,128)S(1)}, f32[8,2048,512]{2,1,0:T(8,128)}) fusion(pred[2048]{0:T(1024)(128)(4,1)S(1)} %fusion.114, bf16[2048,8,64]{0,2,1:T(8,128)(2,1)S(1)} %bitcast.120, bf16[512,8,64]{0,2,1:T(8,128)(2,1)S(1)} %get-tuple-element.295), kind=kOutput, calls=%fused_computation.1.clone.1 | convolution fusion | flops 1098903552 | bytes 36194304 | tf_op jit(solution)/shard_map/while/body/eval_jaxpr/qhd,khd->hqk/dot_general | solution.py:47
  178.6 15.0 %fusion.118 = f32[8,64,512]{2,1,0:T(8,128)S(1)} fusion(bf16[2048,8,64]{0,2,1:T(8,128)(2,1)} %bitcast.121, f32[8,2048,512]{2,1,0:T(8,128)} %get-tuple-element.259, f32[8,512]{1,0:T(8,128)S(1)} %get-tuple-element.289, pred[2048]{0:T(1024)(128)(4,1)S(1)} %fusion.114), kind=kOutput, calls=%fused_computation.7.clone.1 | convolution fusion | flops 1115684864 | bytes 36718592 | tf_op jit(solution)/shard_map/while/body/eval_jaxpr/hqk,khd->qhd/dot_general | solution.py:55
  194.0 15.7 %fusion.116 = f32[8,512]{1,0:T(8,128)S(1)} fusion(f32[8,2048,512]{2,1,0:T(8,128)} %get-tuple-element.259, f32[8,512]{1,0:T(8,128)S(1)} %get-tuple-element.289, pred[2048]{0:T(1024)(128)(4,1)S(1)} %fusion.114), kind=kLoop, calls=%fused_computation.6.clone.1 | loop fusion | flops 41938944 | bytes 33589248 | tf_op jit(solution)/shard_map/while/body/eval_jaxpr/reduce_sum | solution.py:54
  211.0 4.0 constant_dynamic-slice_fusion.3
  215.1 14.4 %bitcast_reduce_fusion.2 = (f32[8,512]{1,0:T(8,128)S(1)}, f32[8,2048,512]{2,1,0:T(8,128)}) fusion(pred[2048]{0:T(1024)(128)(4,1)S(1)} %fusion.114, bf16[2048,8,64]{0,2,1:T(8,128)(2,1)S(1)} %bitcast.120, bf16[512,8,64]{0,2,1:T(8,128)(2,1)S(1)} %get-tuple-element.295), kind=kOutput, calls=%fused_computation.1.clone.1 | convolution fusion | flops 1098903552 | bytes 36194304 | tf_op jit(solution)/shard_map/while/body/eval_jaxpr/qhd,khd->hqk/dot_general | solution.py:47
  229.6 15.0 %fusion.118 = f32[8,64,512]{2,1,0:T(8,128)S(1)} fusion(bf16[2048,8,64]{0,2,1:T(8,128)(2,1)} %bitcast.121, f32[8,2048,512]{2,1,0:T(8,128)} %get-tuple-element.259, f32[8,512]{1,0:T(8,128)S(1)} %get-tuple-element.289, pred[2048]{0:T(1024)(128)(4,1)S(1)} %fusion.114), kind=kOutput, calls=%fused_computation.7.clone.1 | convolution fusion | flops 1115684864 | bytes 36718592 | tf_op jit(solution)/shard_map/while/body/eval_jaxpr/hqk,khd->qhd/dot_general | solution.py:55
  244.9 15.7 %fusion.116 = f32[8,512]{1,0:T(8,128)S(1)} fusion(f32[8,2048,512]{2,1,0:T(8,128)} %get-tuple-element.259, f32[8,512]{1,0:T(8,128)S(1)} %get-tuple-element.289, pred[2048]{0:T(1024)(128)(4,1)S(1)} %fusion.114), kind=kLoop, calls=%fused_computation.6.clone.1 | loop fusion | flops 41938944 | bytes 33589248 | tf_op jit(solution)/shard_map/while/body/eval_jaxpr/reduce_sum | solution.py:54
  261.9 4.0 constant_dynamic-slice_fusion.3
  266.1 14.4 %bitcast_reduce_fusion.2 = (f32[8,512]{1,0:T(8,128)S(1)}, f32[8,2048,512]{2,1,0:T(8,128)}) fusion(pred[2048]{0:T(1024)(128)(4,1)S(1)} %fusion.114, bf16[2048,8,64]{0,2,1:T(8,128)(2,1)S(1)} %bitcast.120, bf16[512,8,64]{0,2,1:T(8,128)(2,1)S(1)} %get-tuple-element.295), kind=kOutput, calls=%fused_computation.1.clone.1 | convolution fusion | flops 1098903552 | bytes 36194304 | tf_op jit(solution)/shard_map/while/body/eval_jaxpr/qhd,khd->hqk/dot_general | solution.py:47
  280.5 15.0 %fusion.118 = f32[8,64,512]{2,1,0:T(8,128)S(1)} fusion(bf16[2048,8,64]{0,2,1:T(8,128)(2,1)} %bitcast.121, f32[8,2048,512]{2,1,0:T(8,128)} %get-tuple-element.259, f32[8,512]{1,0:T(8,128)S(1)} %get-tuple-element.289, pred[2048]{0:T(1024)(128)(4,1)S(1)} %fusion.114), kind=kOutput, calls=%fused_computation.7.clone.1 | convolution fusion | flops 1115684864 | bytes 36718592 | tf_op jit(solution)/shard_map/while/body/eval_jaxpr/hqk,khd->qhd/dot_general | solution.py:55
  295.9 15.7 %fusion.116 = f32[8,512]{1,0:T(8,128)S(1)} fusion(f32[8,2048,512]{2,1,0:T(8,128)} %get-tuple-element.259, f32[8,512]{1,0:T(8,128)S(1)} %get-tuple-element.289, pred[2048]{0:T(1024)(128)(4,1)S(1)} %fusion.114), kind=kLoop, calls=%fused_computation.6.clone.1 | loop fusion | flops 41938944 | bytes 33589248 | tf_op jit(solution)/shard_map/while/body/eval_jaxpr/reduce_sum | solution.py:54
  312.9 4.0 constant_dynamic-slice_fusion.3
  317.0 14.4 %bitcast_reduce_fusion.2 = (f32[8,512]{1,0:T(8,128)S(1)}, f32[8,2048,512]{2,1,0:T(8,128)}) fusion(pred[2048]{0:T(1024)(128)(4,1)S(1)} %fusion.114, bf16[2048,8,64]{0,2,1:T(8,128)(2,1)S(1)} %bitcast.120, bf16[512,8,64]{0,2,1:T(8,128)(2,1)S(1)} %get-tuple-element.295), kind=kOutput, calls=%fused_computation.1.clone.1 | convolution fusion | flops 1098903552 | bytes 36194304 | tf_op jit(solution)/shard_map/while/body/eval_jaxpr/qhd,khd->hqk/dot_general | solution.py:47
  331.4 15.0 %fusion.118 = f32[8,64,512]{2,1,0:T(8,128)S(1)} fusion(bf16[2048,8,64]{0,2,1:T(8,128)(2,1)} %bitcast.121, f32[8,2048,512]{2,1,0:T(8,128)} %get-tuple-element.259, f32[8,512]{1,0:T(8,128)S(1)} %get-tuple-element.289, pred[2048]{0:T(1024)(128)(4,1)S(1)} %fusion.114), kind=kOutput, calls=%fused_computation.7.clone.1 | convolution fusion | flops 1115684864 | bytes 36718592 | tf_op jit(solution)/shard_map/while/body/eval_jaxpr/hqk,khd->qhd/dot_general | solution.py:55
  346.8 15.7 %fusion.116 = f32[8,512]{1,0:T(8,128)S(1)} fusion(f32[8,2048,512]{2,1,0:T(8,128)} %get-tuple-element.259, f32[8,512]{1,0:T(8,128)S(1)} %get-tuple-element.289, pred[2048]{0:T(1024)(128)(4,1)S(1)} %fusion.114), kind=kLoop, calls=%fused_computation.6.clone.1 | loop fusion | flops 41938944 | bytes 33589248 | tf_op jit(solution)/shard_map/while/body/eval_jaxpr/reduce_sum | solution.py:54
  363.9 2.9 convolution_convert_fusion.2
  367.1 38.2 %all-reduce.5.cloned.1.call-done = bf16[512,1024]{1,0:T(8,128)(2,1)} async-done(((bf16[512,1024]{1,0:T(8,128)(2,1)}), bf16[512,1024]{1,0:T(8,128)(2,1)}) %all-reduce.5.cloned.1.call-update) | async-done | bytes 1048592 | tf_op jit(solution)/shard_map/psum | solution.py:139
  407.3 5.9 fusion.34
  413.2 7.9 %convolution_convert_fusion = bf16[512,1024]{1,0:T(8,128)(2,1)} fusion(bf16[1408,1024]{1,0:T(8,128)(2,1)S(1)} %copy-done, f32[512,1408]{1,0:T(8,128)} %fusion.34, bf16[2,1024,1408]{2,1,0:T(8,128)(2,1)} %param.24, bf16[512,1024]{1,0:T(8,128)(2,1)} %all-reduce.5.cloned.1.call-done, bf16[512,1024]{1,0:T(8,128)(2,1)} %param.19, f32[1024]{0:T(1024)S(1)} %copy-done.13, ...), kind=kOutput, calls=%fused_computation.77 | convolution fusion | flops 2963668992 | bytes 11802624 | tf_op jit(solution)/shard_map/dot_general | solution.py:71
  425.2 36.1 %all-reduce.7.cloned.1.call-done = bf16[512,1024]{1,0:T(8,128)(2,1)} async-done(((bf16[512,1024]{1,0:T(8,128)(2,1)}), bf16[512,1024]{1,0:T(8,128)(2,1)}) %all-reduce.7.cloned.1.call-update) | async-done | bytes 1048592 | tf_op jit(solution)/shard_map/psum | solution.py:144
  467.9 5.2 fusion.19
  473.0 61.0 %pmax.7 = f32[8,512]{1,0:T(8,128)S(1)} all-reduce(f32[8,512]{1,0:T(8,128)S(1)} %get-tuple-element.193), channel_id=1, replica_groups=mesh['seq'=16,'head'=2] {'seq'}, use_global_device_ids=true, to_apply=%region_13.14 | all-reduce | flops 4096 | bytes 32768 | tf_op jit(solution)/shard_map/pmax | solution.py:168
  534.1 6.4 fusion.45
  540.6 4.7 fusion.20
  545.3 30.1 %psum.38 = bf16[512,8]{0,1:T(8,128)(2,1)S(1)} all-reduce(bf16[512,8]{0,1:T(8,128)(2,1)S(1)} %bitcast.127), channel_id=1, replica_groups=mesh['seq'=16,'head'=2] {'seq'}, use_global_device_ids=true, to_apply=%region_16.17 | all-reduce | flops 4096 | bytes 16384 | tf_op jit(solution)/shard_map/psum | solution.py:180
  575.4 52.5 %all-reduce.9.cloned.1.call-done = bf16[512,512]{0,1:T(8,128)(2,1)} async-done(((bf16[512,512]{0,1:T(8,128)(2,1)}), bf16[512,512]{0,1:T(8,128)(2,1)}) %all-reduce.9.cloned.1.call-update) | async-done | bytes 524304 | tf_op jit(solution)/shard_map/psum | solution.py:181
  629.0 2.9 convolution_convert_fusion.1
  635.2 37.5 %all-reduce.11.cloned.1.call-done = bf16[512,1024]{1,0:T(8,128)(2,1)} async-done(((bf16[512,1024]{1,0:T(8,128)(2,1)}), bf16[512,1024]{1,0:T(8,128)(2,1)}) %all-reduce.11.cloned.1.call-update) | async-done | bytes 1048592 | tf_op jit(solution)/shard_map/psum | solution.py:187
  (116 shorter events, 35.5 us)
Async XLA Ops:
  7.2 406.0 %copy-start = (bf16[1408,1024]{1,0:T(8,128)(2,1)S(1)}, bf16[1408,1024]{1,0:T(8,128)(2,1)}, u32[]{:S(2)}) copy-start(bf16[1408,1024]{1,0:T(8,128)(2,1)} %param.25) | copy-start | bytes 8650756
  7.2 4.1 copy-start.12
  7.2 140.1 %all-gather.2.cloned.1.call-start = ((), (), s32[]{:S(2)}) async-start(), calls=%async_computation | async-start | bytes 17825792 | tf_op jit(solution)/shard_map/all_gather | solution.py:109
  7.2 4.1 copy-start.3
  14.5 390.8 %all-reduce.5.cloned.1.call-start = ((), (), s32[]{:S(2)}) async-start(), calls=%async_computation.1 | async-start | bytes 2097152 | tf_op jit(solution)/shard_map/psum | solution.py:139
  17.0 141.9 %copy-start.8 = (s32[16]{0:T(128)S(1)}, s32[16]{0:T(128)}, u32[]{:S(2)}) copy-start(s32[16]{0:T(128)} %param.27) | copy-start | bytes 196
  178.6 15.0 %copy-start.1 = (f32[512,512]{0,1:T(8,128)S(1)}, f32[512,512]{0,1:T(8,128)}, u32[]{:S(2)}) copy-start(f32[512,512]{0,1:T(8,128)} %get-tuple-element.278) | copy-start | bytes 3145732 | tf_op jit(solution)/shard_map/while
  194.0 15.7 %copy-start.2 = (f32[512,512]{0,1:T(8,128)}, f32[512,512]{0,1:T(8,128)S(1)}, u32[]{:S(2)}) copy-start(f32[512,512]{0,1:T(8,128)S(1)} %bitcast_add_fusion.2) | copy-start | bytes 3145732 | tf_op jit(solution)/shard_map/while
  229.6 15.0 %copy-start.1 = (f32[512,512]{0,1:T(8,128)S(1)}, f32[512,512]{0,1:T(8,128)}, u32[]{:S(2)}) copy-start(f32[512,512]{0,1:T(8,128)} %get-tuple-element.278) | copy-start | bytes 3145732 | tf_op jit(solution)/shard_map/while
  244.9 15.7 %copy-start.2 = (f32[512,512]{0,1:T(8,128)}, f32[512,512]{0,1:T(8,128)S(1)}, u32[]{:S(2)}) copy-start(f32[512,512]{0,1:T(8,128)S(1)} %bitcast_add_fusion.2) | copy-start | bytes 3145732 | tf_op jit(solution)/shard_map/while
  280.5 15.0 %copy-start.1 = (f32[512,512]{0,1:T(8,128)S(1)}, f32[512,512]{0,1:T(8,128)}, u32[]{:S(2)}) copy-start(f32[512,512]{0,1:T(8,128)} %get-tuple-element.278) | copy-start | bytes 3145732 | tf_op jit(solution)/shard_map/while
  295.8 15.7 %copy-start.2 = (f32[512,512]{0,1:T(8,128)}, f32[512,512]{0,1:T(8,128)S(1)}, u32[]{:S(2)}) copy-start(f32[512,512]{0,1:T(8,128)S(1)} %bitcast_add_fusion.2) | copy-start | bytes 3145732 | tf_op jit(solution)/shard_map/while
  331.4 15.0 %copy-start.1 = (f32[512,512]{0,1:T(8,128)S(1)}, f32[512,512]{0,1:T(8,128)}, u32[]{:S(2)}) copy-start(f32[512,512]{0,1:T(8,128)} %get-tuple-element.278) | copy-start | bytes 3145732 | tf_op jit(solution)/shard_map/while
  346.8 15.7 %copy-start.2 = (f32[512,512]{0,1:T(8,128)}, f32[512,512]{0,1:T(8,128)S(1)}, u32[]{:S(2)}) copy-start(f32[512,512]{0,1:T(8,128)S(1)} %bitcast_add_fusion.2) | copy-start | bytes 3145732 | tf_op jit(solution)/shard_map/while
  363.9 43.4 %copy-start.13 = (f32[1024]{0:T(1024)S(1)}, f32[1024]{0:T(1024)}, u32[]{:S(2)}) copy-start(f32[1024]{0:T(1024)} %param.23) | copy-start | bytes 12292
  366.9 94.5 %all-reduce.7.cloned.1.call-start = ((), (), s32[]{:S(2)}) async-start(), calls=%async_computation.2 | async-start | bytes 2097152 | tf_op jit(solution)/shard_map/psum | solution.py:144
  413.2 9.6 %copy-start.14 = (f32[1024]{0:T(1024)S(1)}, f32[1024]{0:T(1024)}, u32[]{:S(2)}) copy-start(f32[1024]{0:T(1024)} %param.30) | copy-start | bytes 12292
  421.1 206.8 %all-reduce.9.cloned.1.call-start = ((), (), s32[]{:S(2)}) async-start(), calls=%async_computation.3 | async-start | bytes 1048576 | tf_op jit(solution)/shard_map/psum | solution.py:181
  422.8 41.1 %copy-start.10 = (f32[1024]{0:T(1024)S(1)}, f32[1024]{0:T(1024)}, u32[]{:S(2)}) copy-start(f32[1024]{0:T(1024)} %param.26) | copy-start | bytes 12292
  461.3 2.6 copy-start.4
  461.3 2.6 copy-start.5
  461.3 2.8 copy-start.6
  463.9 1.7 copy-start.11
  465.5 2.3 copy-start.7
  540.5 132.2 %all-reduce.11.cloned.1.call-start = ((), (), s32[]{:S(2)}) async-start(), calls=%async_computation.4 | async-start | bytes 2097152 | tf_op jit(solution)/shard_map/psum | solution.py:187
  545.2 86.8 %copy-start.9 = (s32[4]{0:T(128)S(1)}, s32[4]{0:T(128)}, u32[]{:S(2)}) copy-start(s32[4]{0:T(128)} %param.29) | copy-start | bytes 52
Sparse Core Ops, SparseCore 0:
  14.6 132.6 all-gather.1
  367.0 38.2 all-reduce.4
  421.2 40.0 all-reduce.6
  540.6 87.1 all-reduce.8
  632.1 40.5 all-reduce.10
